TPU v7x, 32 devices: a whole 2x2x4 slice. The times are simulated.
32 devices in a mesh: row: 4 (over y, x), col: 2 (over core), depth: 4 (over z).
Axes of the slice: x: 2, y: 2, z: 4, core: 2. Of those that a mesh axis runs over, the one named last changes fastest.
Arguments:
- a_cols: float32 [4096, 1024], P(('row', 'col')), may hold values from -16 to 24, as said below
- past_panels: float32 [4096, 2048], P(('row', 'col'), 'depth'), may hold values from -1 to 1
Outputs:
- factor: float32 [4096, 1024], P(('row', 'col'))
Inputs may be any that keep to these rules, and one draw needn't show every extreme that they name: a_cols minus past_panels times the transpose of the top 1024 rows of past_panels is the first 1024 columns of a symmetric positive definite matrix whose top block has eigenvalues between 2 and 12.
All inputs are finite; a program needn't handle non-finite values.
Results may differ from a plain program's by a relative error of at most 0.0001.
Values sent between devices are 32-bit elements.
A program may use at most 64 MiB of HBM per device.

v0:
```python
import jax
import jax.numpy as jnp
from jax import lax
from jax.sharding import PartitionSpec as P

NB = 512
STEPS = 2


def spread(array, axis, root):
    mine = lax.axis_index(axis) == root
    return lax.psum(jnp.where(mine, array, jnp.zeros_like(array)), axis)


def outer_rows(left, right):
    return lax.dot_general(
        left,
        right,
        (((1,), (1,)), ((), ())),
        precision=lax.Precision.HIGHEST,
        preferred_element_type=jnp.float32,
    )


def body(a_cols, past_panels):
    local_rows = a_cols.shape[0]
    position = lax.axis_index(("row", "col"))
    row_ids = position * local_rows + lax.broadcasted_iota(jnp.int32, (local_rows, NB), 0)
    col_ids = lax.broadcasted_iota(jnp.int32, (local_rows, NB), 1)
    result = jnp.zeros(a_cols.shape, jnp.float32)
    for section in range(STEPS):
        start = section * NB
        root = start // local_rows
        above = spread(past_panels, ("row", "col"), root)
        partial_value = outer_rows(past_panels, above)
        if section > 0:
            layer = lax.axis_index("depth")
            owned_ids = [layer + 0]
            owned_cols = [
                lax.dynamic_slice_in_dim(result, jnp.minimum(index, section - 1) * NB, NB, 1)
                for index in owned_ids
            ]
            sent_rows = jnp.stack([block for block in owned_cols])
            got_rows = spread(sent_rows, ("row", "col"), root)
            weight = (owned_ids[0] < section).astype(jnp.float32)
            partial_value = partial_value + weight * outer_rows(owned_cols[0], got_rows[0])
        summed = lax.psum(partial_value, "depth")
        update = a_cols[:, start : start + NB] - summed
        block = spread(update, ("row", "col"), root)
        diag_factor = jnp.linalg.cholesky(block)
        solved = jax.scipy.linalg.solve_triangular(diag_factor, update.T, lower=True).T
        new_panel = jnp.where(row_ids >= start + col_ids, solved, jnp.float32(0.0))
        result = result.at[:, start : start + NB].set(new_panel)
    return result


def solution(mesh):
    in_specs = (P(("row", "col"), None), P(("row", "col"), "depth"))
    out_specs = P(("row", "col"), None)
    return jax.shard_map(body, mesh=mesh, in_specs=in_specs, out_specs=out_specs, check_vma=False)
```

profile of v0, /device:TPU:0, one launch (start us, length us, event | category | flops | bytes accessed | tf_op | source)
XLA Modules:
  0.0 672.5 jit_solution(3477876616623234303)
XLA Ops:
  6.5 1.6 copy.4
  8.1 1.7 broadcast_select_fusion.3
  9.8 60.1 %all-reduce.10.cloned.1.call-done = f32[512,512]{0,1:T(8,128)} async-done(((f32[512,512]{0,1:T(8,128)}), f32[512,512]{0,1:T(8,128)}) %all-reduce.10.cloned.1.call-update) | async-done | bytes 1048592 | tf_op jit(solution)/shard_map/psum | solution.py:12
  69.9 5.7 convolution_bitcast_fusion.1
  75.7 2.7 fusion.69
  78.8 48.2 %all-reduce.12.cloned.1.call-done = f32[512,512]{0,1:T(8,128)} async-done(((f32[512,512]{0,1:T(8,128)}), f32[512,512]{0,1:T(8,128)}) %all-reduce.12.cloned.1.call-update) | async-done | bytes 1048592 | tf_op jit(solution)/shard_map/psum | solution.py:47
  127.0 2.8 broadcast_select_fusion.2
  129.9 1.0 compare_reduce_fusion.8
  130.8 55.3 %all-reduce.14.cloned.1.call-done = f32[512,512]{0,1:T(8,128)} async-done(((f32[512,512]{0,1:T(8,128)}), f32[512,512]{0,1:T(8,128)}) %all-reduce.14.cloned.1.call-update) | async-done | bytes 1048592 | tf_op jit(solution)/shard_map/psum | solution.py:12
  186.1 1.6 copy.5
  188.0 1.0 copy-done.7
  189.0 11.7 %cholesky.286 = f32[128,128]{1,0:T(8,128)S(1)} custom-call(f32[128,128]{1,0:T(8,128)S(1)} %cholesky.426), custom_call_target="Cholesky" | custom-call | tf_op jit(solution)/shard_map/jit(cholesky)/cholesky | solution.py:50
  200.8 9.8 %custom-call.27 = f32[1,128,128]{1,2,0:T(8,128)S(1)} custom-call(f32[1,128,128]{2,1,0:T(8,128)S(1)} %get-tuple-element.96), custom_call_target="InvertDiagBlocksLowerTriangular" | custom-call | tf_op jit(solution)/shard_map/jit(cholesky)/cholesky | solution.py:50
  210.7 1.2 constant_dynamic-update-slice_fusion.5
  212.0 1.3 convolution_subtract_fusion.7
  213.2 11.7 %cholesky.305 = f32[128,128]{1,0:T(8,128)S(1)} custom-call(f32[128,128]{1,0:T(8,128)S(1)} %cholesky.430), custom_call_target="Cholesky" | custom-call | tf_op jit(solution)/shard_map/jit(cholesky)/cholesky | solution.py:50
  225.0 10.3 %custom-call.28 = f32[1,128,128]{1,2,0:T(8,128)S(1)} custom-call(f32[1,128,128]{2,1,0:T(8,128)S(1)} %get-tuple-element.93), custom_call_target="InvertDiagBlocksLowerTriangular" | custom-call | tf_op jit(solution)/shard_map/jit(cholesky)/cholesky | solution.py:50
  235.6 1.3 convolution_subtract_fusion.9
  236.9 11.7 %cholesky.326 = f32[128,128]{1,0:T(8,128)S(1)} custom-call(f32[128,128]{1,0:T(8,128)S(1)} %cholesky.435), custom_call_target="Cholesky" | custom-call | tf_op jit(solution)/shard_map/jit(cholesky)/cholesky | solution.py:50
  249.2 9.8 %custom-call.29 = f32[1,128,128]{1,2,0:T(8,128)S(1)} custom-call(f32[1,128,128]{2,1,0:T(8,128)S(1)} %get-tuple-element.90), custom_call_target="InvertDiagBlocksLowerTriangular" | custom-call | tf_op jit(solution)/shard_map/jit(cholesky)/cholesky | solution.py:50
  259.3 1.2 convolution_subtract_fusion.11
  260.5 11.7 %cholesky.343 = f32[128,128]{1,0:T(8,128)S(1)} custom-call(f32[128,128]{1,0:T(8,128)S(1)} %convolution_subtract_fusion.11), custom_call_target="Cholesky" | custom-call | tf_op jit(solution)/shard_map/jit(cholesky)/cholesky | solution.py:50
  276.0 1.3 select_select_fusion.1
  277.3 11.1 %while.6 = (s32[]{:T(128)}, f32[512,512]{1,0:T(8,128)}, s32[4,2]{0,1:T(2,128)S(1)}, f32[4,128,128]{2,1,0:T(8,128)S(1)}, s32[]{:T(128)}) while((s32[]{:T(128)}, f32[512,512]{1,0:T(8,128)}, s32[4,2]{0,1:T(2,128)S(1)}, f32[4,128,128]{2,1,0:T(8,128)S(1)}, s32[]{:T(128)}) %tuple.63), condition=%wide.while_cond.2, body=%wide.while_body.2.sunk | while | flops 2 | bytes 131181 | solution.py:51
  278.0 2.2 bitcast_dynamic-update-slice_fusion.4
  280.7 2.2 bitcast_dynamic-update-slice_fusion.4
  283.5 2.2 bitcast_dynamic-update-slice_fusion.4
  286.3 2.1 bitcast_dynamic-update-slice_fusion.4
  288.4 39.3 %custom-call.30 = f32[4,128,128]{1,2,0:T(8,128)S(1)} custom-call(f32[4,128,128]{2,1,0:T(8,128)S(1)} %get-tuple-element.45), custom_call_target="InvertDiagBlocksLowerTriangular" | custom-call | tf_op jit(solution)/shard_map/jit(_solve_triangular)/triangular_solve | solution.py:51
  328.2 1.2 convolution_subtract_fusion.3
  329.8 1.3 convolution_subtract_fusion.2
  331.6 1.6 convolution_subtract_fusion.5
  333.6 0.7 fusion.2
  334.3 1.2 fusion.6
  335.6 61.2 %all-reduce.20.cloned.1.call-done = (f32[512,512]{0,1:T(8,128)}, f32[512,512]{0,1:T(8,128)}) async-done(((f32[512,512]{0,1:T(8,128)}, f32[512,512]{0,1:T(8,128)}), (f32[512,512]{0,1:T(8,128)}, f32[512,512]{0,1:T(8,128)})) %all-reduce.20.cloned.1.call-update) | async-done | bytes 2097168 | tf_op jit(solution)/shard_map/psum | solution.py:12
  396.8 4.8 convolution_bitcast_fusion
  401.6 2.9 fusion
  405.1 50.5 %all-reduce.16.cloned.1.call-done = f32[512,512]{0,1:T(8,128)} async-done(((f32[512,512]{0,1:T(8,128)}), f32[512,512]{0,1:T(8,128)}) %all-reduce.16.cloned.1.call-update) | async-done | bytes 1048592 | tf_op jit(solution)/shard_map/psum | solution.py:47
  455.6 2.8 broadcast_select_fusion
  458.4 56.2 %all-reduce.18.cloned.1.call-done = f32[512,512]{0,1:T(8,128)} async-done(((f32[512,512]{0,1:T(8,128)}), f32[512,512]{0,1:T(8,128)}) %all-reduce.18.cloned.1.call-update) | async-done | bytes 1048592 | tf_op jit(solution)/shard_map/psum | solution.py:12
  514.6 1.6 copy.9
  516.5 1.0 copy-done.6
  517.5 11.7 %cholesky.358 = f32[128,128]{1,0:T(8,128)S(1)} custom-call(f32[128,128]{1,0:T(8,128)S(1)} %cholesky.439), custom_call_target="Cholesky" | custom-call | tf_op jit(solution)/shard_map/jit(cholesky)/cholesky | solution.py:50
  529.4 9.8 %custom-call.31 = f32[1,128,128]{1,2,0:T(8,128)S(1)} custom-call(f32[1,128,128]{2,1,0:T(8,128)S(1)} %get-tuple-element.86), custom_call_target="InvertDiagBlocksLowerTriangular" | custom-call | tf_op jit(solution)/shard_map/jit(cholesky)/cholesky | solution.py:50
  539.2 1.2 constant_dynamic-update-slice_fusion.3
  540.4 1.3 convolution_subtract_fusion.6
  541.7 11.7 %cholesky.377 = f32[128,128]{1,0:T(8,128)S(1)} custom-call(f32[128,128]{1,0:T(8,128)S(1)} %cholesky.443), custom_call_target="Cholesky" | custom-call | tf_op jit(solution)/shard_map/jit(cholesky)/cholesky | solution.py:50
  554.8 10.2 %custom-call.32 = f32[1,128,128]{1,2,0:T(8,128)S(1)} custom-call(f32[1,128,128]{2,1,0:T(8,128)S(1)} %get-tuple-element.83), custom_call_target="InvertDiagBlocksLowerTriangular" | custom-call | tf_op jit(solution)/shard_map/jit(cholesky)/cholesky | solution.py:50
  565.3 1.3 convolution_subtract_fusion.8
  566.6 11.7 %cholesky.398 = f32[128,128]{1,0:T(8,128)S(1)} custom-call(f32[128,128]{1,0:T(8,128)S(1)} %cholesky.448), custom_call_target="Cholesky" | custom-call | tf_op jit(solution)/shard_map/jit(cholesky)/cholesky | solution.py:50
  579.0 9.8 %custom-call.33 = f32[1,128,128]{1,2,0:T(8,128)S(1)} custom-call(f32[1,128,128]{2,1,0:T(8,128)S(1)} %get-tuple-element.80), custom_call_target="InvertDiagBlocksLowerTriangular" | custom-call | tf_op jit(solution)/shard_map/jit(cholesky)/cholesky | solution.py:50
  589.0 1.2 convolution_subtract_fusion.10
  590.3 11.8 %cholesky.415 = f32[128,128]{1,0:T(8,128)S(1)} custom-call(f32[128,128]{1,0:T(8,128)S(1)} %convolution_subtract_fusion.10), custom_call_target="Cholesky" | custom-call | tf_op jit(solution)/shard_map/jit(cholesky)/cholesky | solution.py:50
  605.3 1.1 select_select_fusion
  606.4 11.7 %while.7 = (s32[]{:T(128)}, f32[512,512]{1,0:T(8,128)}, s32[4,2]{0,1:T(2,128)S(1)}, f32[4,128,128]{2,1,0:T(8,128)S(1)}, s32[]{:T(128)}) while((s32[]{:T(128)}, f32[512,512]{1,0:T(8,128)}, s32[4,2]{0,1:T(2,128)S(1)}, f32[4,128,128]{2,1,0:T(8,128)S(1)}, s32[]{:T(128)}) %tuple.82), condition=%wide.while_cond.2.clone, body=%wide.while_body.2.clone.sunk | while | flops 2 | bytes 131181 | solution.py:51
  607.1 2.3 bitcast_dynamic-update-slice_fusion.5
  610.0 2.3 bitcast_dynamic-update-slice_fusion.5
  613.0 2.3 bitcast_dynamic-update-slice_fusion.5
  615.9 2.2 bitcast_dynamic-update-slice_fusion.5
  618.1 39.3 %custom-call.34 = f32[4,128,128]{1,2,0:T(8,128)S(1)} custom-call(f32[4,128,128]{2,1,0:T(8,128)S(1)} %get-tuple-element.46), custom_call_target="InvertDiagBlocksLowerTriangular" | custom-call | tf_op jit(solution)/shard_map/jit(_solve_triangular)/triangular_solve | solution.py:51
  657.9 1.2 convolution_subtract_fusion.1
  659.5 1.3 convolution_subtract_fusion
  661.3 1.6 convolution_subtract_fusion.4
  663.6 1.8 copy.10
  (91 shorter events, 16.6 us)
Async XLA Ops:
  6.5 63.4 %all-reduce.10.cloned.1.call-start = ((), (), s32[]{:S(2)}) async-start(), calls=%async_computation | async-start | bytes 2097152 | tf_op jit(solution)/shard_map/psum | solution.py:12
  8.1 61.8 %copy-start = (f32[512,512]{1,0:T(8,128)S(1)}, f32[512,512]{1,0:T(8,128)}, u32[]{:S(2)}) copy-start(f32[512,512]{1,0:T(8,128)} %param.10) | copy-start | bytes 3145732
  9.8 117.2 %all-reduce.12.cloned.1.call-start = ((), (), s32[]{:S(2)}) async-start(), calls=%async_computation.1 | async-start | bytes 2097152 | tf_op jit(solution)/shard_map/psum | solution.py:47
  75.7 110.4 %all-reduce.14.cloned.1.call-start = ((), (), s32[]{:S(2)}) async-start(), calls=%async_computation.2 | async-start | bytes 2097152 | tf_op jit(solution)/shard_map/psum | solution.py:12
  129.8 267.0 %all-reduce.20.cloned.1.call-start = ((), (), s32[]{:S(2)}) async-start(), calls=%async_computation.5 | async-start | bytes 4194304 | tf_op jit(solution)/shard_map/psum | solution.py:12
  186.1 1.7 copy-start.1
  188.0 1.0 copy-start.7
  236.9 90.9 %copy-start.3 = (f32[512,512]{1,0:T(8,128)S(1)}, f32[512,512]{1,0:T(8,128)}, u32[]{:S(2)}) copy-start(f32[512,512]{1,0:T(8,128)} %get-tuple-element.72) | copy-start | bytes 3145732
  335.5 120.1 %all-reduce.16.cloned.1.call-start = ((), (), s32[]{:S(2)}) async-start(), calls=%async_computation.3 | async-start | bytes 2097152 | tf_op jit(solution)/shard_map/psum | solution.py:47
  396.8 4.8 copy-start.8
  401.6 3.2 copy-start.5
  404.5 110.1 %all-reduce.18.cloned.1.call-start = ((), (), s32[]{:S(2)}) async-start(), calls=%async_computation.4 | async-start | bytes 2097152 | tf_op jit(solution)/shard_map/psum | solution.py:12
  514.6 1.7 copy-start.2
  516.5 1.0 copy-start.6
  566.6 90.9 %copy-start.4 = (f32[512,512]{1,0:T(8,128)S(1)}, f32[512,512]{1,0:T(8,128)}, u32[]{:S(2)}) copy-start(f32[512,512]{1,0:T(8,128)} %get-tuple-element.70) | copy-start | bytes 3145732
Sparse Core Ops, SparseCore 0:
  10.5 59.4 all-reduce.9
  75.8 51.1 all-reduce.11
  130.1 55.9 all-reduce.13
  335.6 61.0 all-reduce.19
  404.6 50.9 all-reduce.15
  458.6 55.9 all-reduce.17
where the time goes:
time: 678 us; the launch traced here: 672 us
  waiting for transfers between devices  332 us (49%)
  other arithmetic  250 us (37%)
  matrix products  35.9 us (5%)
  local copies, waits for them, and re-layouts  34.9 us (5%)
  between operations  19.2 us (3%)
    psum x4, waiting for transfers between devices, spread(): return lax.psum(jnp.where(mine, array, jnp.zeros_like(array)), axis)  233 us
    another operation x29, other arithmetic, body(): diag_factor = jnp.linalg.cholesky(block)  158 us
    psum x2, waiting for transfers between devices, body(): summed = lax.psum(partial_value, 'depth')  98.7 us
    another operation x5, other arithmetic, body(): jax.scipy.linalg.solve_triangular(diag_factor, update.T, lower=True)  81 us
    another operation x27, local copies, waits for them, and re-layouts, body(): jax.scipy.linalg.solve_triangular(diag_factor, update.T, lower=True)  22.6 us
  transfers between devices with their start and end apart: 6, of which 6 were waited for; matrix products, arithmetic and copies ran while one was open for 1% of the time, Pallas kernels for 0%

commit v1 on v0

--- a/solution.py
+++ b/solution.py
@@ -44,7 +44,8 @@
             got_rows = spread(sent_rows, ("row", "col"), root)
             weight = (owned_ids[0] < section).astype(jnp.float32)
             partial_value = partial_value + weight * outer_rows(owned_cols[0], got_rows[0])
-        summed = lax.psum(partial_value, "depth")
+        parts = lax.all_gather(partial_value, "depth")
+        summed = jnp.sum(parts, axis=0)
         update = a_cols[:, start : start + NB] - summed
         block = spread(update, ("row", "col"), root)
         diag_factor = jnp.linalg.cholesky(block)

time: 678 us -> 755 us (1.11)
  waiting for transfers between devices: 332 us -> 387 us
  local copies, waits for them, and re-layouts: 34.9 us -> 47.7 us
    all_gather x0 -> x2, waiting for transfers between devices: none -> 157 us  [body(): parts = lax.all_gather(partial_value, 'depth')]
    psum x2 -> x0, waiting for transfers between devices: 98.7 us -> none  [body(): summed = lax.psum(partial_value, 'depth')]
    all_gather x0 -> x2, local copies, waits for them, and re-layouts: none -> 12.4 us  [body(): parts = lax.all_gather(partial_value, 'depth')]
    reduce_sum x0 -> x2, other arithmetic: none -> 9.36 us  [body(): summed = jnp.sum(parts, axis=0)]
where the time goes in v1:
time: 755 us; the launch traced here: 748 us
  waiting for transfers between devices  387 us (51%)
  other arithmetic  257 us (34%)
  local copies, waits for them, and re-layouts  47.7 us (6%)
  matrix products  35.8 us (5%)
  between operations  19.2 us (3%)
    psum x4, waiting for transfers between devices, spread(): return lax.psum(jnp.where(mine, array, jnp.zeros_like(array)), axis)  231 us
    another operation x29, other arithmetic, body(): diag_factor = jnp.linalg.cholesky(block)  158 us
    all_gather x2, waiting for transfers between devices, body(): parts = lax.all_gather(partial_value, 'depth')  157 us
    another operation x5, other arithmetic, body(): jax.scipy.linalg.solve_triangular(diag_factor, update.T, lower=True)  81.1 us
    another operation x27, local copies, waits for them, and re-layouts, body(): jax.scipy.linalg.solve_triangular(diag_factor, update.T, lower=True)  23 us
  transfers between devices with their start and end apart: 6, of which 6 were waited for; matrix products, arithmetic and copies ran while one was open for 1% of the time, Pallas kernels for 0%

profile of v1, /device:TPU:0, one launch (start us, length us, event | category | flops | bytes accessed | tf_op | source)
XLA Modules:
  0.0 747.7 jit_solution(5471993620824718786)
XLA Ops:
  6.5 1.6 copy.4
  8.1 1.7 broadcast_select_fusion.3
  9.9 60.0 %all-reduce.8.cloned.1.call-done = f32[512,512]{0,1:T(8,128)} async-done(((f32[512,512]{0,1:T(8,128)}), f32[512,512]{0,1:T(8,128)}) %all-reduce.8.cloned.1.call-update) | async-done | bytes 1048592 | tf_op jit(solution)/shard_map/psum | solution.py:12
  69.9 5.7 convolution_bitcast_fusion.1
  75.7 2.7 fusion.69
  78.7 77.1 %all-gather.5.cloned.1.call-done = f32[2048,512]{0,1:T(8,128)} async-done(((f32[512,512]{0,1:T(8,128)}), f32[2048,512]{0,1:T(8,128)}) %all-gather.5.cloned.1.call-update) | async-done | bytes 4194320 | tf_op jit(solution)/shard_map/all_gather | solution.py:47
  155.8 6.0 reshape.104
  161.8 4.7 reduce_sum.18
  166.5 1.7 broadcast_select_fusion.2
  169.3 54.2 %all-reduce.10.cloned.1.call-done = f32[512,512]{0,1:T(8,128)} async-done(((f32[512,512]{0,1:T(8,128)}), f32[512,512]{0,1:T(8,128)}) %all-reduce.10.cloned.1.call-update) | async-done | bytes 1048592 | tf_op jit(solution)/shard_map/psum | solution.py:12
  223.5 1.6 copy.5
  226.4 11.7 %cholesky.286 = f32[128,128]{1,0:T(8,128)S(1)} custom-call(f32[128,128]{1,0:T(8,128)S(1)} %cholesky.426), custom_call_target="Cholesky" | custom-call | tf_op jit(solution)/shard_map/jit(cholesky)/cholesky | solution.py:51
  238.2 9.8 %custom-call.27 = f32[1,128,128]{1,2,0:T(8,128)S(1)} custom-call(f32[1,128,128]{2,1,0:T(8,128)S(1)} %get-tuple-element.96), custom_call_target="InvertDiagBlocksLowerTriangular" | custom-call | tf_op jit(solution)/shard_map/jit(cholesky)/cholesky | solution.py:51
  248.1 1.2 constant_dynamic-update-slice_fusion.5
  249.4 1.3 convolution_subtract_fusion.7
  250.7 11.7 %cholesky.305 = f32[128,128]{1,0:T(8,128)S(1)} custom-call(f32[128,128]{1,0:T(8,128)S(1)} %cholesky.430), custom_call_target="Cholesky" | custom-call | tf_op jit(solution)/shard_map/jit(cholesky)/cholesky | solution.py:51
  262.4 10.0 %custom-call.28 = f32[1,128,128]{1,2,0:T(8,128)S(1)} custom-call(f32[1,128,128]{2,1,0:T(8,128)S(1)} %get-tuple-element.93), custom_call_target="InvertDiagBlocksLowerTriangular" | custom-call | tf_op jit(solution)/shard_map/jit(cholesky)/cholesky | solution.py:51
  272.6 1.3 convolution_subtract_fusion.9
  273.9 11.7 %cholesky.326 = f32[128,128]{1,0:T(8,128)S(1)} custom-call(f32[128,128]{1,0:T(8,128)S(1)} %cholesky.435), custom_call_target="Cholesky" | custom-call | tf_op jit(solution)/shard_map/jit(cholesky)/cholesky | solution.py:51
  286.3 9.8 %custom-call.29 = f32[1,128,128]{1,2,0:T(8,128)S(1)} custom-call(f32[1,128,128]{2,1,0:T(8,128)S(1)} %get-tuple-element.90), custom_call_target="InvertDiagBlocksLowerTriangular" | custom-call | tf_op jit(solution)/shard_map/jit(cholesky)/cholesky | solution.py:51
  296.4 1.2 convolution_subtract_fusion.11
  297.6 11.7 %cholesky.343 = f32[128,128]{1,0:T(8,128)S(1)} custom-call(f32[128,128]{1,0:T(8,128)S(1)} %convolution_subtract_fusion.11), custom_call_target="Cholesky" | custom-call | tf_op jit(solution)/shard_map/jit(cholesky)/cholesky | solution.py:51
  313.0 1.4 select_select_fusion.1
  314.4 11.4 %while.6 = (s32[]{:T(128)}, f32[512,512]{1,0:T(8,128)}, s32[4,2]{0,1:T(2,128)S(1)}, f32[4,128,128]{2,1,0:T(8,128)S(1)}, s32[]{:T(128)}) while((s32[]{:T(128)}, f32[512,512]{1,0:T(8,128)}, s32[4,2]{0,1:T(2,128)S(1)}, f32[4,128,128]{2,1,0:T(8,128)S(1)}, s32[]{:T(128)}) %tuple.63), condition=%wide.while_cond.2, body=%wide.while_body.2.sunk | while | flops 2 | bytes 131181 | solution.py:52
  315.1 2.2 bitcast_dynamic-update-slice_fusion.4
  317.9 2.2 bitcast_dynamic-update-slice_fusion.4
  320.8 2.2 bitcast_dynamic-update-slice_fusion.4
  323.7 2.2 bitcast_dynamic-update-slice_fusion.4
  325.8 39.3 %custom-call.30 = f32[4,128,128]{1,2,0:T(8,128)S(1)} custom-call(f32[4,128,128]{2,1,0:T(8,128)S(1)} %get-tuple-element.45), custom_call_target="InvertDiagBlocksLowerTriangular" | custom-call | tf_op jit(solution)/shard_map/jit(_solve_triangular)/triangular_solve | solution.py:52
  365.6 1.2 convolution_subtract_fusion.3
  367.2 1.3 convolution_subtract_fusion.2
  369.0 1.6 convolution_subtract_fusion.5
  371.7 1.2 fusion.6
  372.9 61.2 %all-reduce.14.cloned.1.call-done = (f32[512,512]{0,1:T(8,128)}, f32[512,512]{0,1:T(8,128)}) async-done(((f32[512,512]{0,1:T(8,128)}, f32[512,512]{0,1:T(8,128)}), (f32[512,512]{0,1:T(8,128)}, f32[512,512]{0,1:T(8,128)})) %all-reduce.14.cloned.1.call-update) | async-done | bytes 2097168 | tf_op jit(solution)/shard_map/psum | solution.py:12
  434.1 4.8 convolution_bitcast_fusion
  439.0 2.9 fusion
  442.3 79.5 %all-gather.7.cloned.1.call-done = f32[2048,512]{0,1:T(8,128)} async-done(((f32[512,512]{0,1:T(8,128)}), f32[2048,512]{0,1:T(8,128)}) %all-gather.7.cloned.1.call-update) | async-done | bytes 4194320 | tf_op jit(solution)/shard_map/all_gather | solution.py:47
  521.8 6.4 reshape.105
  528.2 4.7 reduce_sum.19
  532.9 1.6 broadcast_select_fusion
  534.6 55.3 %all-reduce.12.cloned.1.call-done = f32[512,512]{0,1:T(8,128)} async-done(((f32[512,512]{0,1:T(8,128)}), f32[512,512]{0,1:T(8,128)}) %all-reduce.12.cloned.1.call-update) | async-done | bytes 1048592 | tf_op jit(solution)/shard_map/psum | solution.py:12
  589.9 1.6 copy.9
  592.8 11.7 %cholesky.358 = f32[128,128]{1,0:T(8,128)S(1)} custom-call(f32[128,128]{1,0:T(8,128)S(1)} %cholesky.439), custom_call_target="Cholesky" | custom-call | tf_op jit(solution)/shard_map/jit(cholesky)/cholesky | solution.py:51
  604.7 9.8 %custom-call.31 = f32[1,128,128]{1,2,0:T(8,128)S(1)} custom-call(f32[1,128,128]{2,1,0:T(8,128)S(1)} %get-tuple-element.86), custom_call_target="InvertDiagBlocksLowerTriangular" | custom-call | tf_op jit(solution)/shard_map/jit(cholesky)/cholesky | solution.py:51
  614.5 1.2 constant_dynamic-update-slice_fusion.3
  615.7 1.3 convolution_subtract_fusion.6
  617.0 11.9 %cholesky.377 = f32[128,128]{1,0:T(8,128)S(1)} custom-call(f32[128,128]{1,0:T(8,128)S(1)} %cholesky.443), custom_call_target="Cholesky" | custom-call | tf_op jit(solution)/shard_map/jit(cholesky)/cholesky | solution.py:51
  630.3 9.8 %custom-call.32 = f32[1,128,128]{1,2,0:T(8,128)S(1)} custom-call(f32[1,128,128]{2,1,0:T(8,128)S(1)} %get-tuple-element.83), custom_call_target="InvertDiagBlocksLowerTriangular" | custom-call | tf_op jit(solution)/shard_map/jit(cholesky)/cholesky | solution.py:51
  640.3 1.3 convolution_subtract_fusion.8
  641.7 11.7 %cholesky.398 = f32[128,128]{1,0:T(8,128)S(1)} custom-call(f32[128,128]{1,0:T(8,128)S(1)} %cholesky.448), custom_call_target="Cholesky" | custom-call | tf_op jit(solution)/shard_map/jit(cholesky)/cholesky | solution.py:51
  654.1 9.8 %custom-call.33 = f32[1,128,128]{1,2,0:T(8,128)S(1)} custom-call(f32[1,128,128]{2,1,0:T(8,128)S(1)} %get-tuple-element.80), custom_call_target="InvertDiagBlocksLowerTriangular" | custom-call | tf_op jit(solution)/shard_map/jit(cholesky)/cholesky | solution.py:51
  664.1 1.2 convolution_subtract_fusion.10
  665.3 11.9 %cholesky.415 = f32[128,128]{1,0:T(8,128)S(1)} custom-call(f32[128,128]{1,0:T(8,128)S(1)} %convolution_subtract_fusion.10), custom_call_target="Cholesky" | custom-call | tf_op jit(solution)/shard_map/jit(cholesky)/cholesky | solution.py:51
  680.5 1.1 select_select_fusion
  681.6 11.7 %while.7 = (s32[]{:T(128)}, f32[512,512]{1,0:T(8,128)}, s32[4,2]{0,1:T(2,128)S(1)}, f32[4,128,128]{2,1,0:T(8,128)S(1)}, s32[]{:T(128)}) while((s32[]{:T(128)}, f32[512,512]{1,0:T(8,128)}, s32[4,2]{0,1:T(2,128)S(1)}, f32[4,128,128]{2,1,0:T(8,128)S(1)}, s32[]{:T(128)}) %tuple.82), condition=%wide.while_cond.2.clone, body=%wide.while_body.2.clone.sunk | while | flops 2 | bytes 131181 | solution.py:52
  682.3 2.3 bitcast_dynamic-update-slice_fusion.5
  685.2 2.3 bitcast_dynamic-update-slice_fusion.5
  688.1 2.3 bitcast_dynamic-update-slice_fusion.5
  691.1 2.2 bitcast_dynamic-update-slice_fusion.5
  693.3 39.3 %custom-call.34 = f32[4,128,128]{1,2,0:T(8,128)S(1)} custom-call(f32[4,128,128]{2,1,0:T(8,128)S(1)} %get-tuple-element.46), custom_call_target="InvertDiagBlocksLowerTriangular" | custom-call | tf_op jit(solution)/shard_map/jit(_solve_triangular)/triangular_solve | solution.py:52
  733.0 1.2 convolution_subtract_fusion.1
  734.7 1.3 convolution_subtract_fusion
  736.5 1.6 convolution_subtract_fusion.4
  738.8 1.8 copy.10
  (95 shorter events, 20.2 us)
Async XLA Ops:
  6.5 63.4 %all-reduce.8.cloned.1.call-start = ((), (), s32[]{:S(2)}) async-start(), calls=%async_computation | async-start | bytes 2097152 | tf_op jit(solution)/shard_map/psum | solution.py:12
  8.1 61.8 %copy-start = (f32[512,512]{1,0:T(8,128)S(1)}, f32[512,512]{1,0:T(8,128)}, u32[]{:S(2)}) copy-start(f32[512,512]{1,0:T(8,128)} %param.10) | copy-start | bytes 3145732
  9.9 145.9 %all-gather.5.cloned.1.call-start = ((), (), s32[]{:S(2)}) async-start(), calls=%async_computation.3 | async-start | bytes 5242880 | tf_op jit(solution)/shard_map/all_gather | solution.py:47
  75.6 147.9 %all-reduce.10.cloned.1.call-start = ((), (), s32[]{:S(2)}) async-start(), calls=%async_computation.1 | async-start | bytes 2097152 | tf_op jit(solution)/shard_map/psum | solution.py:12
  168.2 266.0 %all-reduce.14.cloned.1.call-start = ((), (), s32[]{:S(2)}) async-start(), calls=%async_computation.5 | async-start | bytes 4194304 | tf_op jit(solution)/shard_map/psum | solution.py:12
  223.5 1.7 copy-start.1
  225.4 1.0 copy-start.7
  273.9 91.2 %copy-start.3 = (f32[512,512]{1,0:T(8,128)S(1)}, f32[512,512]{1,0:T(8,128)}, u32[]{:S(2)}) copy-start(f32[512,512]{1,0:T(8,128)} %get-tuple-element.72) | copy-start | bytes 3145732
  372.9 148.9 %all-gather.7.cloned.1.call-start = ((), (), s32[]{:S(2)}) async-start(), calls=%async_computation.4 | async-start | bytes 5242880 | tf_op jit(solution)/shard_map/all_gather | solution.py:47
  434.1 4.8 copy-start.8
  438.9 3.0 copy-start.5
  441.9 148.0 %all-reduce.12.cloned.1.call-start = ((), (), s32[]{:S(2)}) async-start(), calls=%async_computation.2 | async-start | bytes 2097152 | tf_op jit(solution)/shard_map/psum | solution.py:12
  589.9 1.7 copy-start.2
  591.8 1.0 copy-start.6
  641.6 91.0 %copy-start.4 = (f32[512,512]{1,0:T(8,128)S(1)}, f32[512,512]{1,0:T(8,128)}, u32[]{:S(2)}) copy-start(f32[512,512]{1,0:T(8,128)} %get-tuple-element.70) | copy-start | bytes 3145732
Sparse Core Ops, SparseCore 0:
  10.5 59.4 all-reduce.7
  75.8 79.9 all-gather.4
  168.3 55.1 all-reduce.9
  373.0 61.0 all-reduce.13
  442.0 79.7 all-gather.6
  534.7 55.1 all-reduce.11
